TPU v7x, 256 devices: a whole 4x4x8 slice. The times are simulated.
256 devices in a mesh: tm: 128 (over y, x, z), head: 2 (over core).
Axes of the slice: x: 4, y: 4, z: 8, core: 2. Of those that a mesh axis runs over, the one named last changes fastest.
Arguments:
- queries: bfloat16 [16384, 4096], P('tm', 'head'), may hold values from -6 to 6
- keys: bfloat16 [16384, 4096], P('tm', 'head'), may hold values from -6 to 6
- values: bfloat16 [16384, 4096], P('tm', 'head'), may hold values from -6 to 6
- segment: int32 [16384], P('tm'), may hold values from 0 to 1, never falling along the last dimension, each value on 1 to 14336 neighbouring positions
- level_weight: float32 [15, 32, 16384], P(None, 'head', 'tm'), may hold values from 0.16 to 6
- gain: float32 [4096], P('head'), may hold values from 0.1 to 1.9
- grad_out: bfloat16 [16384, 4096], P('tm', 'head'), may hold values from -6 to 6
Outputs:
- normed: bfloat16 [16384, 4096], P('tm', 'head')
- grad_queries: bfloat16 [16384, 4096], P('tm', 'head')
- grad_keys: bfloat16 [16384, 4096], P('tm', 'head')
- grad_values: bfloat16 [16384, 4096], P('tm', 'head')
- grad_level: float32 [15, 32, 16384], P(None, 'head', 'tm')
Inputs may be any that keep to these rules, and one draw needn't show every extreme that they name: segment numbers never fall along the sequence; each of the two segments holds 2048 to 14336 neighbouring positions.
All inputs are finite; a program needn't handle non-finite values.
Results may differ from a plain program's by a relative error of at most 0.0055.
Values sent between devices are 32-bit elements; how exact they have to be, the bound alone decides.
A program may use at most 128 MiB of HBM per device.

v0:
```python
import jax
import jax.numpy as jnp
from jax import lax
from jax.sharding import PartitionSpec as P

EPSILON = 1e-05
PRECISE = lax.Precision.HIGHEST


def from_behind(value, axis, steps):
    count = lax.axis_size(axis)
    leading, last = (max(0, -steps), min(count, count - steps))
    return lax.ppermute(value, axis, [(source, source + steps) for source in range(leading, last)])


def partner(x, axis, apart):
    return lax.ppermute(x, axis, [(i, i ^ 1 << apart) for i in range(lax.axis_size(axis))])


def level_table(tokens):
    places = jnp.arange(tokens, dtype=jnp.int32)
    crossed = jnp.bitwise_xor(places[:, None], places[None, :])
    levels = jnp.zeros((tokens, tokens), jnp.int32)
    for offset in range(tokens.bit_length() - 1):
        levels = levels + (jnp.right_shift(crossed, offset) > 0).astype(jnp.int32)
    return (levels, places[:, None] >= places[None, :])


def per_device(queries, keys, values, segment, level_weight, gain, grad_out):
    tokens = queries.shape[0]
    head_count = level_weight.shape[1]
    head_width = queries.shape[1] // head_count
    total_levels = level_weight.shape[0]
    local_levels = tokens.bit_length()
    log_tm = lax.axis_size("tm").bit_length() - 1
    features = queries.shape[1] * lax.axis_size("head")
    position = lax.axis_index("tm")
    levels, causal = level_table(tokens)
    level_scale = jnp.exp2(-jnp.maximum(jnp.arange(total_levels) - 1, 0).astype(jnp.float32) / 2.0)
    scaled = level_weight * level_scale[:, None, None]
    shape3 = (tokens, head_count, head_width)
    query_heads = queries.reshape(shape3)
    key_heads = keys.reshape(shape3)
    value_heads = values.reshape(shape3)
    same_segment = (segment[:, None] == segment[None, :]) & causal
    level_onehot = jnp.where(
        (levels[None] == jnp.arange(local_levels, dtype=jnp.int32)[:, None, None])
        & same_segment[None],
        jnp.float32(1.0),
        jnp.float32(0.0),
    )
    weight = jnp.einsum("lht,lts->hts", scaled[:local_levels], level_onehot, precision=PRECISE)
    scores = jnp.einsum("thd,shd->hts", query_heads, key_heads, preferred_element_type=jnp.float32)
    near_terms = (scores * weight).astype(jnp.bfloat16)
    mixed_out = jnp.einsum(
        "hts,shd->thd", near_terms, value_heads, preferred_element_type=jnp.float32
    )
    keep_rows = segment == segment[-1]
    kept_keys = jnp.where(keep_rows[:, None, None], key_heads, jnp.zeros_like(key_heads))
    aggregate = jnp.einsum(
        "shd,she->hde", kept_keys, value_heads, preferred_element_type=jnp.float32
    )
    state_gate = segment[-1:].astype(jnp.float32)
    buckets = []
    gate_values = []
    uppers = []
    joins = []
    sent_states = []
    for level_bit in range(log_tm):
        is_upper = jnp.right_shift(position, level_bit) % 2 == 1
        sent_states.append(aggregate)
        if level_bit == log_tm - 1:
            got_state, got_gate = from_behind((aggregate, state_gate), "tm", 1 << level_bit)
        else:
            got_state, got_gate = partner((aggregate, state_gate), "tm", level_bit)
        same_gate = jnp.where(got_gate[0] == state_gate[0], jnp.float32(1.0), jnp.float32(0.0))
        buckets.append(got_state)
        gate_values.append(got_gate[0])
        uppers.append(is_upper)
        joins.append(same_gate)
        if level_bit < log_tm - 1:
            aggregate = jnp.where(
                is_upper, aggregate + same_gate * got_state, got_state + same_gate * aggregate
            )
            state_gate = jnp.where(is_upper, state_gate, got_gate)
    query_float = query_heads.astype(jnp.float32)
    segment_float = segment.astype(jnp.float32)
    reaches = []
    weighted_all = []
    for level_bit in range(log_tm):
        reach_mask = jnp.where(
            uppers[level_bit] & (segment_float == gate_values[level_bit]),
            jnp.float32(1.0),
            jnp.float32(0.0),
        )
        weighted = reach_mask[:, None] * scaled[local_levels + level_bit].T
        remote_read = jnp.einsum("thd,hde->the", query_float, buckets[level_bit], precision=PRECISE)
        mixed_out = mixed_out + remote_read * weighted[:, :, None]
        reaches.append(reach_mask)
        weighted_all.append(weighted)
    flat_out = mixed_out.reshape(tokens, head_count * head_width)
    grad_float = grad_out.astype(jnp.float32)
    squares, project = lax.psum(
        (jnp.sum(flat_out * flat_out, axis=1), jnp.sum(gain * grad_float * flat_out, axis=1)),
        "head",
    )
    radius = jnp.sqrt(squares / features + EPSILON)
    normed = (flat_out / radius[:, None] * gain).astype(jnp.bfloat16)
    grad_mixed = (
        gain * grad_float / radius[:, None] - flat_out * (project / (features * radius**3))[:, None]
    ).astype(jnp.bfloat16)
    grad_heads = grad_mixed.reshape(shape3)
    grad_heads_float = grad_heads.astype(jnp.float32)
    grad_near = jnp.einsum(
        "thd,shd->hts", grad_heads, value_heads, preferred_element_type=jnp.float32
    )
    grad_score = (grad_near * weight).astype(jnp.bfloat16)
    grad_query = jnp.einsum(
        "hts,shd->thd", grad_score, key_heads, preferred_element_type=jnp.float32
    )
    grad_key = jnp.einsum(
        "hts,thd->shd", grad_score, query_heads, preferred_element_type=jnp.float32
    )
    grad_value = jnp.einsum(
        "hts,thd->shd", near_terms, grad_heads, preferred_element_type=jnp.float32
    )
    near_level = jnp.einsum("hts,lts->lht", grad_near * scores, level_onehot, precision=PRECISE)
    level_rows = [near_level[tier_level] for tier_level in range(local_levels)]
    grad_buckets = []
    for level_bit in range(log_tm):
        grad_buckets.append(
            jnp.einsum(
                "thd,the->hde",
                query_float * weighted_all[level_bit][:, :, None],
                grad_heads_float,
                precision=PRECISE,
            )
        )
    remote_rows = {}
    carried = jnp.zeros_like(aggregate)
    for level_bit in reversed(range(log_tm)):
        is_upper = uppers[level_bit]
        same_gate = joins[level_bit]
        outgoing = jnp.where(is_upper, grad_buckets[level_bit] + same_gate * carried, carried)
        staying = jnp.where(is_upper, carried, same_gate * carried)
        incoming, resent = partner((outgoing, sent_states[level_bit]), "tm", level_bit)
        carried = staying + incoming
        grad_query = (
            grad_query
            + jnp.einsum("hde,the->thd", resent, grad_heads_float, precision=PRECISE)
            * weighted_all[level_bit][:, :, None]
        )
        read_back = jnp.einsum("thd,hde->the", query_float, resent, precision=PRECISE)
        remote_rows[level_bit] = (
            reaches[level_bit][None, :] * jnp.sum(read_back * grad_heads_float, axis=2).T
        )
    for level_bit in range(log_tm):
        level_rows.append(remote_rows[level_bit])
    keep_float = keep_rows.astype(jnp.float32)[:, None, None]
    grad_key = grad_key + keep_float * jnp.einsum(
        "hde,she->shd", carried, value_heads.astype(jnp.float32), precision=PRECISE
    )
    grad_value = grad_value + keep_float * jnp.einsum(
        "hde,shd->she", carried, key_heads.astype(jnp.float32), precision=PRECISE
    )
    grad_level = jnp.stack(level_rows) * level_scale[:, None, None]
    width_all = head_count * head_width
    return (
        normed,
        grad_query.astype(jnp.bfloat16).reshape(tokens, width_all),
        grad_key.astype(jnp.bfloat16).reshape(tokens, width_all),
        grad_value.astype(jnp.bfloat16).reshape(tokens, width_all),
        grad_level,
    )


def solution(mesh):
    placed = (
        P("tm", "head"),
        P("tm", "head"),
        P("tm", "head"),
        P("tm"),
        P(None, "head", "tm"),
        P("head"),
        P("tm", "head"),
    )
    return jax.shard_map(
        per_device,
        mesh=mesh,
        in_specs=placed,
        out_specs=(
            P("tm", "head"),
            P("tm", "head"),
            P("tm", "head"),
            P("tm", "head"),
            P(None, "head", "tm"),
        ),
        check_vma=False,
    )
```

profile of v0, /device:TPU:1, one launch (start us, length us, event | category | flops | bytes accessed | tf_op | source)
XLA Modules:
  0.0 505.0 jit_solution(9406150726435704733)
XLA Ops:
  9.7 21.2 %collective-permute-start.1 = (f32[1]{0:T(128)}, f32[1]{0:T(128)}, u32[]{:S(2)}, u32[]{:S(2)}) collective-permute-start(f32[1]{0:T(128)} %convert_element_type.112), channel_id=1, source_target_pairs={{0,2},{2,0},{4,6},{6,4},{8,10},{10,8},{12,14},{14,12},{16,18},{18,... | collective-permute-start | bytes 20 | tf_op jit(solution)/shard_map/ppermute | solution.py:17
  32.9 3.9 collective-permute-start.2
  37.5 20.8 %collective-permute-start.3 = (f32[1]{0:T(128)}, f32[1]{0:T(128)}, u32[]{:S(2)}, u32[]{:S(2)}) collective-permute-start(f32[1]{0:T(128)} %select_n.227), channel_id=1, source_target_pairs={{0,4},{2,6},{4,0},{6,2},{8,12},{10,14},{12,8},{14,10},{16,20},{18,... | collective-permute-start | bytes 20 | tf_op jit(solution)/shard_map/ppermute | solution.py:17
  58.3 23.8 %collective-permute-done.3 = f32[1]{0:T(128)} collective-permute-done((f32[1]{0:T(128)}, f32[1]{0:T(128)}, u32[]{:S(2)}, u32[]{:S(2)}) %collective-permute-start.3) | collective-permute-done | bytes 36 | tf_op jit(solution)/shard_map/ppermute | solution.py:17
  85.5 6.5 %collective-permute-start.4 = (f32[16,128,128]{2,1,0:T(8,128)}, f32[16,128,128]{2,1,0:T(8,128)}, u32[]{:S(2)}, u32[]{:S(2)}) collective-permute-start(f32[16,128,128]{2,1,0:T(8,128)} %add_select_fusion.5), channel_id=1, source_target_pairs={{0,8},{2,10},{4,12},{6,14},{8,0},{10,2},{12,4},{14,6},{16,24},{18,... | collective-permute-start | bytes 3145736 | tf_op jit(solution)/shard_map/ppermute | solution.py:17
  92.6 41.2 %collective-permute-start.5 = (f32[1]{0:T(128)}, f32[1]{0:T(128)}, u32[]{:S(2)}, u32[]{:S(2)}) collective-permute-start(f32[1]{0:T(128)} %select_n.234), channel_id=1, source_target_pairs={{0,8},{2,10},{4,12},{6,14},{8,0},{10,2},{12,4},{14,6},{16,24},{18,... | collective-permute-start | bytes 20 | tf_op jit(solution)/shard_map/ppermute | solution.py:17
  133.9 3.9 collective-permute-done.5
  151.1 12.4 %collective-permute-start.7 = (f32[1]{0:T(128)}, f32[1]{0:T(128)}, u32[]{:S(2)}, u32[]{:S(2)}) collective-permute-start(f32[1]{0:T(128)} %select_n.241), channel_id=1, source_target_pairs={{0,16},{2,18},{4,20},{6,22},{8,24},{10,26},{12,28},{14,30},{16,0},... | collective-permute-start | bytes 20 | tf_op jit(solution)/shard_map/ppermute | solution.py:17
  175.1 16.2 %collective-permute-start.9 = (f32[1]{0:T(128)}, f32[1]{0:T(128)}, u32[]{:S(2)}, u32[]{:S(2)}) collective-permute-start(f32[1]{0:T(128)} %select_n.248), channel_id=1, source_target_pairs={{0,32},{2,34},{4,36},{6,38},{8,40},{10,42},{12,44},{14,46},{16,48}... | collective-permute-start | bytes 20 | tf_op jit(solution)/shard_map/ppermute | solution.py:17
  197.6 5.6 %collective-permute-start.13 = (f32[1]{0:T(128)}, f32[1]{0:T(128)}, u32[]{:S(2)}, u32[]{:S(2)}) collective-permute-start(f32[1]{0:T(128)} %select_n.262), channel_id=1, source_target_pairs={{0,128},{2,130},{4,132},{6,134},{8,136},{10,138},{12,140},{14,142}... | collective-permute-start | bytes 20 | tf_op jit(solution)/shard_map/ppermute | solution.py:13
  203.1 5.1 %and_select_fusion.6 = (f32[128]{0:T(128)S(1)}, f32[128]{0:T(128)}, f32[128]{0:T(128)}, f32[128]{0:T(128)}, f32[128]{0:T(128)}, /*index=5*/f32[128]{0:T(128)S(1)}, f32[128]{0:T(128)S(1)}) fusion(pred[]{:T(512)} %eq.136, s32[128]{0:T(128)S(1)} %copy-done.57, f32[]{:T(128)} %bitcast.5, f32[]{:T(128)} %bitcast.11, pred[]{:T(512)} %eq.140, f32[]{:T(128)} %bitcast.17, ...), kind=kLoop, calls=%fused_computation.178 | loop fusion | flops 2816 | bytes 4131 | tf_op jit(solution)/shard_map/jit(_where)/select_n | solution.py:91
  223.7 8.8 %collective-permute-done.10 = f32[16,128,128]{2,1,0:T(8,128)} collective-permute-done((f32[16,128,128]{2,1,0:T(8,128)}, f32[16,128,128]{2,1,0:T(8,128)}, u32[]{:S(2)}, u32[]{:S(2)}) %collective-permute-start.10) | collective-permute-done | bytes 1048608 | tf_op jit(solution)/shard_map/ppermute | solution.py:17
  234.2 4.8 collective-permute-start.12
  246.0 8.7 %collective-permute-done.12 = f32[16,128,128]{2,1,0:T(8,128)S(1)} collective-permute-done((f32[16,128,128]{2,1,0:T(8,128)S(1)}, f32[16,128,128]{2,1,0:T(8,128)S(1)}, u32[]{:S(2)}, u32[]{:S(2)}) %collective-permute-start.12) | collective-permute-done | bytes 1048608 | tf_op jit(solution)/shard_map/ppermute | solution.py:13
  260.3 9.7 %all-reduce = (f32[128]{0:T(128)S(1)}, f32[128]{0:T(128)S(1)}) all-reduce(f32[128]{0:T(128)S(1)} %get-tuple-element.57, f32[128]{0:T(128)S(1)} %multiply_reduce_fusion), channel_id=1, replica_groups=mesh['tm'=128,'head'=2] {'head'}, use_global_device_ids=true, to_apply=%region_1.2 | all-reduce | flops 256 | bytes 2048 | tf_op jit(solution)/shard_map/psum | solution.py:103
  275.8 4.2 collective-permute-start.15
  280.0 23.5 %collective-permute-done.15 = f32[16,128,128]{2,1,0:T(8,128)} collective-permute-done((f32[16,128,128]{2,1,0:T(8,128)}, f32[16,128,128]{2,1,0:T(8,128)}, u32[]{:S(2)}, u32[]{:S(2)}) %collective-permute-start.15) | collective-permute-done | bytes 1048608 | tf_op jit(solution)/shard_map/ppermute | solution.py:17
  309.7 20.1 %collective-permute-done.16 = f32[16,128,128]{2,1,0:T(8,128)S(1)} collective-permute-done((f32[16,128,128]{2,1,0:T(8,128)S(1)}, f32[16,128,128]{2,1,0:T(8,128)S(1)}, u32[]{:S(2)}, u32[]{:S(2)}) %collective-permute-start.16) | collective-permute-done | bytes 1048608 | tf_op jit(solution)/shard_map/ppermute | solution.py:17
  340.4 15.5 %collective-permute-done.17 = f32[16,128,128]{2,1,0:T(8,128)S(1)} collective-permute-done((f32[16,128,128]{2,1,0:T(8,128)S(1)}, f32[16,128,128]{2,1,0:T(8,128)S(1)}, u32[]{:S(2)}, u32[]{:S(2)}) %collective-permute-start.17) | collective-permute-done | bytes 1048608 | tf_op jit(solution)/shard_map/ppermute | solution.py:17
  364.5 13.5 %collective-permute-done.18 = f32[16,128,128]{2,1,0:T(8,128)S(1)} collective-permute-done((f32[16,128,128]{2,1,0:T(8,128)S(1)}, f32[16,128,128]{2,1,0:T(8,128)S(1)}, u32[]{:S(2)}, u32[]{:S(2)}) %collective-permute-start.18) | collective-permute-done | bytes 1048608 | tf_op jit(solution)/shard_map/ppermute | solution.py:17
  388.3 33.1 %collective-permute-done.19 = f32[16,128,128]{2,1,0:T(8,128)S(1)} collective-permute-done((f32[16,128,128]{2,1,0:T(8,128)S(1)}, f32[16,128,128]{2,1,0:T(8,128)S(1)}, u32[]{:S(2)}, u32[]{:S(2)}) %collective-permute-start.19) | collective-permute-done | bytes 1048608 | tf_op jit(solution)/shard_map/ppermute | solution.py:17
  433.9 31.8 %collective-permute-done.20 = f32[16,128,128]{2,1,0:T(8,128)} collective-permute-done((f32[16,128,128]{2,1,0:T(8,128)}, f32[16,128,128]{2,1,0:T(8,128)}, u32[]{:S(2)}, u32[]{:S(2)}) %collective-permute-start.20) | collective-permute-done | bytes 1048608 | tf_op jit(solution)/shard_map/ppermute | solution.py:17
  481.2 13.0 %collective-permute-done.21 = f32[16,128,128]{2,1,0:T(8,128)} collective-permute-done((f32[16,128,128]{2,1,0:T(8,128)}, f32[16,128,128]{2,1,0:T(8,128)}, u32[]{:S(2)}, u32[]{:S(2)}) %collective-permute-start.21) | collective-permute-done | bytes 1048608 | tf_op jit(solution)/shard_map/ppermute | solution.py:17
  494.3 3.3 fusion.25
  (262 shorter events, 143.8 us)
Async XLA Ops:
  6.5 25.1 %collective-permute-start = (f32[16,128,128]{2,1,0:T(8,128)S(1)}, f32[16,128,128]{2,1,0:T(8,128)S(1)}, u32[]{:S(2)}, u32[]{:S(2)}) collective-permute-start(f32[16,128,128]{2,1,0:T(8,128)S(1)} %fusion.51), channel_id=1, source_target_pairs={{0,2},{2,0},{4,6},{6,4},{8,10},{10,8},{12,14},{14,12},{16,18},{18,... | collective-permute-start | bytes 3145736 | tf_op jit(solution)/shard_map/ppermute | solution.py:17
  9.7 21.2 %collective-permute-start.1 = (f32[1]{0:T(128)}, f32[1]{0:T(128)}, u32[]{:S(2)}, u32[]{:S(2)}) collective-permute-start(f32[1]{0:T(128)} %convert_element_type.112), channel_id=1, source_target_pairs={{0,2},{2,0},{4,6},{6,4},{8,10},{10,8},{12,14},{14,12},{16,18},{18,... | collective-permute-start | bytes 20 | tf_op jit(solution)/shard_map/ppermute | solution.py:17
  31.6 189.8 %copy-start.3 = (f32[16,128,128]{2,1,0:T(8,128)}, f32[16,128,128]{2,1,0:T(8,128)S(1)}, u32[]{:S(2)}) copy-start(f32[16,128,128]{2,1,0:T(8,128)S(1)} %collective-permute-done) | copy-start | bytes 3145732
  32.9 49.8 %collective-permute-start.2 = (f32[16,128,128]{2,1,0:T(8,128)}, f32[16,128,128]{2,1,0:T(8,128)S(1)}, u32[]{:S(2)}, u32[]{:S(2)}) collective-permute-start(f32[16,128,128]{2,1,0:T(8,128)} %add_select_fusion.6), channel_id=1, source_target_pairs={{0,4},{2,6},{4,0},{6,2},{8,12},{10,14},{12,8},{14,10},{16,20},{18,... | collective-permute-start | bytes 3145736 | tf_op jit(solution)/shard_map/ppermute | solution.py:17
  37.5 44.6 %collective-permute-start.3 = (f32[1]{0:T(128)}, f32[1]{0:T(128)}, u32[]{:S(2)}, u32[]{:S(2)}) collective-permute-start(f32[1]{0:T(128)} %select_n.227), channel_id=1, source_target_pairs={{0,4},{2,6},{4,0},{6,2},{8,12},{10,14},{12,8},{14,10},{16,20},{18,... | collective-permute-start | bytes 20 | tf_op jit(solution)/shard_map/ppermute | solution.py:17
  85.5 52.9 %collective-permute-start.4 = (f32[16,128,128]{2,1,0:T(8,128)}, f32[16,128,128]{2,1,0:T(8,128)}, u32[]{:S(2)}, u32[]{:S(2)}) collective-permute-start(f32[16,128,128]{2,1,0:T(8,128)} %add_select_fusion.5), channel_id=1, source_target_pairs={{0,8},{2,10},{4,12},{6,14},{8,0},{10,2},{12,4},{14,6},{16,24},{18,... | collective-permute-start | bytes 3145736 | tf_op jit(solution)/shard_map/ppermute | solution.py:17
  92.6 45.1 %collective-permute-start.5 = (f32[1]{0:T(128)}, f32[1]{0:T(128)}, u32[]{:S(2)}, u32[]{:S(2)}) collective-permute-start(f32[1]{0:T(128)} %select_n.234), channel_id=1, source_target_pairs={{0,8},{2,10},{4,12},{6,14},{8,0},{10,2},{12,4},{14,6},{16,24},{18,... | collective-permute-start | bytes 20 | tf_op jit(solution)/shard_map/ppermute | solution.py:17
  141.2 23.9 %collective-permute-start.6 = (f32[16,128,128]{2,1,0:T(8,128)}, f32[16,128,128]{2,1,0:T(8,128)S(1)}, u32[]{:S(2)}, u32[]{:S(2)}) collective-permute-start(f32[16,128,128]{2,1,0:T(8,128)} %add_select_fusion.4), channel_id=1, source_target_pairs={{0,16},{2,18},{4,20},{6,22},{8,24},{10,26},{12,28},{14,30},{16,0},... | collective-permute-start | bytes 3145736 | tf_op jit(solution)/shard_map/ppermute | solution.py:17
  151.1 13.2 %collective-permute-start.7 = (f32[1]{0:T(128)}, f32[1]{0:T(128)}, u32[]{:S(2)}, u32[]{:S(2)}) collective-permute-start(f32[1]{0:T(128)} %select_n.241), channel_id=1, source_target_pairs={{0,16},{2,18},{4,20},{6,22},{8,24},{10,26},{12,28},{14,30},{16,0},... | collective-permute-start | bytes 20 | tf_op jit(solution)/shard_map/ppermute | solution.py:17
  168.4 42.0 %collective-permute-start.8 = (f32[16,128,128]{2,1,0:T(8,128)}, f32[16,128,128]{2,1,0:T(8,128)S(1)}, u32[]{:S(2)}, u32[]{:S(2)}) collective-permute-start(f32[16,128,128]{2,1,0:T(8,128)} %add_select_fusion.3), channel_id=1, source_target_pairs={{0,32},{2,34},{4,36},{6,38},{8,40},{10,42},{12,44},{14,46},{16,48}... | collective-permute-start | bytes 3145736 | tf_op jit(solution)/shard_map/ppermute | solution.py:17
  175.1 17.1 %collective-permute-start.9 = (f32[1]{0:T(128)}, f32[1]{0:T(128)}, u32[]{:S(2)}, u32[]{:S(2)}) collective-permute-start(f32[1]{0:T(128)} %select_n.248), channel_id=1, source_target_pairs={{0,32},{2,34},{4,36},{6,38},{8,40},{10,42},{12,44},{14,46},{16,48}... | collective-permute-start | bytes 20 | tf_op jit(solution)/shard_map/ppermute | solution.py:17
  193.6 2.6 collective-permute-start.11
  197.6 5.6 %collective-permute-start.13 = (f32[1]{0:T(128)}, f32[1]{0:T(128)}, u32[]{:S(2)}, u32[]{:S(2)}) collective-permute-start(f32[1]{0:T(128)} %select_n.262), channel_id=1, source_target_pairs={{0,128},{2,130},{4,132},{6,134},{8,136},{10,138},{12,140},{14,142}... | collective-permute-start | bytes 20 | tf_op jit(solution)/shard_map/ppermute | solution.py:13
  212.8 19.6 %collective-permute-start.10 = (f32[16,128,128]{2,1,0:T(8,128)}, f32[16,128,128]{2,1,0:T(8,128)}, u32[]{:S(2)}, u32[]{:S(2)}) collective-permute-start(f32[16,128,128]{2,1,0:T(8,128)} %add_select_fusion.2), channel_id=1, source_target_pairs={{0,64},{2,66},{4,68},{6,70},{8,72},{10,74},{12,76},{14,78},{16,80}... | collective-permute-start | bytes 3145736 | tf_op jit(solution)/shard_map/ppermute | solution.py:17
  220.5 135.4 %copy-start.44 = (f32[128,16]{0,1:T(8,128)}, f32[128,16]{0,1:T(8,128)S(1)}, u32[]{:S(2)}) copy-start(f32[128,16]{0,1:T(8,128)S(1)} %copy.227) | copy-start | bytes 24580
  234.2 20.5 %collective-permute-start.12 = (f32[16,128,128]{2,1,0:T(8,128)S(1)}, f32[16,128,128]{2,1,0:T(8,128)S(1)}, u32[]{:S(2)}, u32[]{:S(2)}) collective-permute-start(f32[16,128,128]{2,1,0:T(8,128)S(1)} %add_select_fusion.1), channel_id=1, source_target_pairs={{0,128},{2,130},{4,132},{6,134},{8,136},{10,138},{12,140},{14,142}... | collective-permute-start | bytes 3145736 | tf_op jit(solution)/shard_map/ppermute | solution.py:13
  275.8 27.7 %collective-permute-start.15 = (f32[16,128,128]{2,1,0:T(8,128)}, f32[16,128,128]{2,1,0:T(8,128)}, u32[]{:S(2)}, u32[]{:S(2)}) collective-permute-start(f32[16,128,128]{2,1,0:T(8,128)} %add_select_fusion), channel_id=1, source_target_pairs={{0,128},{2,130},{4,132},{6,134},{8,136},{10,138},{12,140},{14,142}... | collective-permute-start | bytes 3145736 | tf_op jit(solution)/shard_map/ppermute | solution.py:17
  306.0 23.9 %collective-permute-start.16 = (f32[16,128,128]{2,1,0:T(8,128)S(1)}, f32[16,128,128]{2,1,0:T(8,128)S(1)}, u32[]{:S(2)}, u32[]{:S(2)}) collective-permute-start(f32[16,128,128]{2,1,0:T(8,128)S(1)} %fusion.5), channel_id=1, source_target_pairs={{0,64},{2,66},{4,68},{6,70},{8,72},{10,74},{12,76},{14,78},{16,80}... | collective-permute-start | bytes 3145736 | tf_op jit(solution)/shard_map/ppermute | solution.py:17
  306.4 74.7 %collective-permute-start.14 = (f32[16,128,128]{2,1,0:T(8,128)S(1)}, f32[16,128,128]{2,1,0:T(8,128)S(1)}, u32[]{:S(2)}, u32[]{:S(2)}) collective-permute-start(f32[16,128,128]{2,1,0:T(8,128)S(1)} %copy-done.40), channel_id=1, source_target_pairs={{0,128},{2,130},{4,132},{6,134},{8,136},{10,138},{12,140},{14,142}... | collective-permute-start | bytes 3145736 | tf_op jit(solution)/shard_map/ppermute | solution.py:17
  332.8 23.1 %collective-permute-start.17 = (f32[16,128,128]{2,1,0:T(8,128)S(1)}, f32[16,128,128]{2,1,0:T(8,128)S(1)}, u32[]{:S(2)}, u32[]{:S(2)}) collective-permute-start(f32[16,128,128]{2,1,0:T(8,128)S(1)} %fusion.4), channel_id=1, source_target_pairs={{0,32},{2,34},{4,36},{6,38},{8,40},{10,42},{12,44},{14,46},{16,48}... | collective-permute-start | bytes 3145736 | tf_op jit(solution)/shard_map/ppermute | solution.py:17
  357.2 20.8 %collective-permute-start.18 = (f32[16,128,128]{2,1,0:T(8,128)S(1)}, f32[16,128,128]{2,1,0:T(8,128)S(1)}, u32[]{:S(2)}, u32[]{:S(2)}) collective-permute-start(f32[16,128,128]{2,1,0:T(8,128)S(1)} %fusion.3), channel_id=1, source_target_pairs={{0,16},{2,18},{4,20},{6,22},{8,24},{10,26},{12,28},{14,30},{16,0},... | collective-permute-start | bytes 3145736 | tf_op jit(solution)/shard_map/ppermute | solution.py:17
  379.5 41.9 %collective-permute-start.19 = (f32[16,128,128]{2,1,0:T(8,128)S(1)}, f32[16,128,128]{2,1,0:T(8,128)S(1)}, u32[]{:S(2)}, u32[]{:S(2)}) collective-permute-start(f32[16,128,128]{2,1,0:T(8,128)S(1)} %fusion.2), channel_id=1, source_target_pairs={{0,8},{2,10},{4,12},{6,14},{8,0},{10,2},{12,4},{14,6},{16,24},{18,... | collective-permute-start | bytes 3145736 | tf_op jit(solution)/shard_map/ppermute | solution.py:17
  423.6 42.1 %collective-permute-start.20 = (f32[16,128,128]{2,1,0:T(8,128)}, f32[16,128,128]{2,1,0:T(8,128)}, u32[]{:S(2)}, u32[]{:S(2)}) collective-permute-start(f32[16,128,128]{2,1,0:T(8,128)} %fusion.1), channel_id=1, source_target_pairs={{0,4},{2,6},{4,0},{6,2},{8,12},{10,14},{12,8},{14,10},{16,20},{18,... | collective-permute-start | bytes 3145736 | tf_op jit(solution)/shard_map/ppermute | solution.py:17
  469.5 24.7 %collective-permute-start.21 = (f32[16,128,128]{2,1,0:T(8,128)}, f32[16,128,128]{2,1,0:T(8,128)}, u32[]{:S(2)}, u32[]{:S(2)}) collective-permute-start(f32[16,128,128]{2,1,0:T(8,128)} %fusion), channel_id=1, source_target_pairs={{0,2},{2,0},{4,6},{6,4},{8,10},{10,8},{12,14},{14,12},{16,18},{18,... | collective-permute-start | bytes 3145736 | tf_op jit(solution)/shard_map/ppermute | solution.py:17
  (73 other events, 664.9 us)
where the time goes:
time: 515 us; the launch traced here: 505 us
  waiting for transfers between devices  198 us (38%)
  starting transfers between devices  157 us (30%)
  matrix products  61.4 us (12%)
  other arithmetic  34.8 us (7%)
  local copies, waits for them, and re-layouts  33.8 us (7%)
  between operations  10.8 us (2%)
  blocking collectives  9.69 us (2%)
    ppermute x20, waiting for transfers between devices, partner(): lax.ppermute(x, axis, [(i, i ^ 1 << apart) for i in range(lax.axis_size(a...  189 us
    ppermute x20, starting transfers between devices, partner(): lax.ppermute(x, axis, [(i, i ^ 1 << apart) for i in range(lax.axis_size(a...  146 us
    unnamed x157, local copies, waits for them, and re-layouts  19.1 us
    dot_general x7, matrix products, per_device(): jnp.einsum('hde,the->thd', resent, grad_heads_float, precision=PRECISE)  15.1 us
    select_n x6, other arithmetic, per_device(): jnp.where(is_upper, aggregate + same_gate * got_state, got_state + same_g...  13.4 us
    dot_general x7, matrix products, per_device(): jnp.einsum('thd,the->hde', query_float * weighted_all[level_bit][:, :, No...  12.9 us
    dot_general x7, matrix products, per_device(): jnp.einsum('thd,hde->the', query_float, buckets[level_bit], precision=PRE...  11.5 us
    ppermute x2, starting transfers between devices, from_behind(): lax.ppermute(value, axis, [(source, source + steps) for source in range(l...  10.3 us
  transfers between devices with their start and end apart: 22, of which 14 were waited for; matrix products, arithmetic and copies ran while one was open for 15% of the time, Pallas kernels for 0%

commit v1 on v0

v1 whole, which is shorter than its diff:
```python
import functools
import jax
import jax.numpy as jnp
from jax import lax
from jax.experimental import pallas as pl
from jax.experimental.pallas import tpu as pltpu
from jax.sharding import PartitionSpec as P

MESH = pl.DeviceIdType.MESH
F32 = jnp.float32
BF16 = jnp.bfloat16
EPSILON = 1e-05
TOK = 128
WIDTH = 128
NH = 16
BITS = 7
NEAR_LEVELS = 8
LEVELS = NEAR_LEVELS + BITS
FEATURES = 4096
UP_LAG = (0, 3, 7, 10, 12, 14, 16)
DOWN_LAG = (0, 1, 3, 5, 7, 9, 11, 13, 15, 17)


def dot(a, b, left, right):
    return lax.dot_general(a, b, (((left,), (right,)), ((), ())), preferred_element_type=F32)


def place():
    tm = lax.axis_index("tm")
    z = lax.rem(tm, 8)
    x = lax.rem(lax.div(tm, 8), 4)
    y = lax.div(tm, 32)
    inner = lax.rem(lax.div(z + 1, 2), 2)
    near = tm + 1 - 2 * lax.rem(z, 2)
    across = tm - z + inner * (8 * lax.div(z, 4) + 3 - z) + (1 - inner) * (7 - z)
    x_one = tm + 8 * (1 - 2 * lax.rem(x, 2))
    x_three = tm + 8 * (3 - 2 * x)
    y_one = tm + 32 * (1 - 2 * lax.rem(y, 2))
    y_three = tm + 32 * (3 - 2 * y)
    bits = (
        lax.rem(z, 2), lax.rem(lax.div(z, 2), 2), lax.div(z, 4),
        lax.rem(x, 2), lax.div(x, 2), lax.rem(y, 2), lax.div(y, 2),
    )
    return inner, (near, across, x_one, x_three, y_one, y_three), bits


def remote(src, dst, send, recv, other):
    return pltpu.make_async_remote_copy(
        src_ref=src, dst_ref=dst, send_sem=send, recv_sem=recv,
        device_id=other, device_id_type=MESH,
    )


def body(
    q, k, v, g, lw, rows, table, keep, gain,
    normed, gq, gk, gv, gl,
    tails, recv, agg, grecv, gagg, reach, q_t, near, score, weight, mixed, sums, sums_got,
    gm, o, got, got_join, cur, gkp, gvp,
    ssem, rsem, lsem, gss, grs, gls, dssem, drsem, jss, jrs, xss, xrs,
):
    inner, partners, bits = place()
    near_by, across, x_one, x_three, y_one, y_three = partners
    other_core = {"head": 1 - lax.axis_index("head")}
    target = tuple(
        {"tm": p} for p in (near_by, across, across, x_one, x_three, y_one, y_three)
    )
    is_inner = inner == 1
    is_outer = inner == 0
    upper = tuple(bit == 1 for bit in bits)
    lower = tuple(bit == 0 for bit in bits)
    upper_f = tuple(bit.astype(F32) for bit in bits)

    barrier = pltpu.get_barrier_semaphore()
    for p in partners:
        pl.semaphore_signal(barrier, inc=1, device_id={"tm": p}, device_id_type=MESH)
    pl.semaphore_signal(barrier, inc=1, device_id=other_core, device_id_type=MESH)
    pl.semaphore_wait(barrier, 7)

    def cols(h):
        return pl.ds(pl.multiple_of(h * WIDTH, WIDTH), WIDTH)

    def only(b, fn):
        if b == 1:
            pl.when(is_inner)(fn)
        elif b == 2:
            pl.when(is_outer)(fn)
        else:
            fn()

    def up_copy(b, h):
        src = tails.at[h] if b == 0 else agg.at[b - 1, h]
        return remote(src, recv.at[b, h], ssem.at[b, h], rsem.at[b, h], target[b])

    def up_relay(b, h):
        return remote(recv.at[b, h], recv.at[b, h], lsem.at[h], rsem.at[b, h], target[0])

    def gate_copy(b):
        return remote(gagg.at[b], grecv.at[b], gss.at[b], grs.at[b], target[b])

    def gate_relay(b):
        return remote(grecv.at[b], grecv.at[b], gls, grs.at[b], target[0])

    gagg[0] = rows[0]
    gate_copy(0).start()

    @pl.loop(0, NH)
    def _(h):
        kept = k[:, cols(h)].astype(F32) * keep[...]
        tails[h] = dot(kept.astype(BF16), v[:, cols(h)], 0, 0)
        up_copy(0, h).start()

    def near_forward(h):
        query = q[:, cols(h)]
        s = dot(k[:, cols(h)], query, 1, 1)
        level = table[...]
        w = jnp.zeros((TOK, TOK), F32)
        for l in range(NEAR_LEVELS):
            w = jnp.where(level == float(l), lw[h, l:l + 1, :], w)
        terms = (s * w).astype(BF16)
        score[h] = s
        weight[h] = w
        near[h] = terms
        q_t[h] = query.T
        mixed[h] = dot(terms, v[:, cols(h)], 0, 0)

    def up_event(b, h):
        @pl.when(h == 0)
        def _():
            gate_copy(b).wait_recv()
            if b in (1, 2):
                only(b, lambda: gate_relay(b).start())
            if b < BITS - 1:
                gagg[b + 1] = gagg[b] * upper_f[b] + grecv[b] * (1.0 - upper_f[b])
                only(b + 1, lambda: gate_copy(b + 1).start())
            hit = jnp.where(rows[1, 0:1, :] == grecv[b, 0:1, :], 1.0, 0.0)
            reach[b:b + 1, :] = hit * upper_f[b]

        up_copy(b, h).wait_recv()
        if b in (1, 2):
            only(b, lambda: up_relay(b, h).start())
        if b < BITS - 1:
            same = jnp.where(grecv[b, 0:1, :] == gagg[b, 0:1, :], 1.0, 0.0)
            mine_by = upper_f[b] + (1.0 - upper_f[b]) * same
            got_by = (1.0 - upper_f[b]) + upper_f[b] * same
            mine = tails[h] if b == 0 else agg[b - 1, h]
            agg[b, h] = mine * mine_by + recv[b, h] * got_by
            only(b + 1, lambda: up_copy(b + 1, h).start())

    def far_read(h):
        by = lw[h, 8:16, :] * reach[...]
        by_t = by.T
        query = q[:, cols(h)].astype(F32)
        for b in range(BITS):
            @pl.when(upper[b])
            def _(b=b):
                scaled_q = (query * by_t[:, b:b + 1]).astype(BF16)
                mixed[h] = mixed[h] + dot(scaled_q, recv[b, h].astype(BF16), 1, 0)
        m = mixed[h]
        sums[0] = sums[0] + m * m
        sums[1] = sums[1] + m * g[:, cols(h)].astype(F32) * gain[:, cols(h)]

    sums[...] = jnp.zeros_like(sums)
    reach[...] = jnp.zeros_like(reach)

    @pl.loop(0, NH + UP_LAG[-1])
    def _(step):
        for b in range(BITS):
            h = step - UP_LAG[b]

            @pl.when((h >= 0) & (h < NH))
            def _(b=b, h=h):
                up_event(b, h)

        @pl.when(step < NH)
        def _():
            near_forward(step)

        h = step - UP_LAG[-1]

        @pl.when(h >= 0)
        def _():
            far_read(h)

    swap = remote(sums, sums_got, xss, xrs, other_core)
    swap.start()
    swap.wait_recv()
    squares = jnp.sum(sums[0] + sums_got[0], axis=1, keepdims=True)
    project = jnp.sum(sums[1] + sums_got[1], axis=1, keepdims=True)
    radius = jnp.sqrt(squares / FEATURES + EPSILON)
    inverse = 1.0 / radius
    pull = project * inverse * inverse * inverse / FEATURES

    def down_copy(b, h):
        return remote(o.at[b, h], got.at[b, h], dssem.at[b, h], drsem.at[b, h], target[b])

    def join(b, h):
        return remote(o.at[b, h], got_join.at[h], jss.at[h], jrs.at[h], target[0])

    def far_row(b, h):
        return lw[h, 8 + b:9 + b, :] * reach[b:b + 1, :]

    def far_grad(b, h):
        scaled_q = (q_t[h].astype(F32) * far_row(b, h)).astype(BF16)
        return dot(scaled_q, gm[h], 1, 0)

    def split(b, h):
        same = jnp.where(grecv[b, 0:1, :] == gagg[b, 0:1, :], 1.0, 0.0)

        @pl.when(upper[b])
        def _():
            o[b, h] = cur[h] * same + far_grad(b, h)

        @pl.when(lower[b])
        def _():
            o[b, h] = cur[h]
            cur[h] = cur[h] * same

    def emit(h):
        m = mixed[h]
        scale = gain[:, cols(h)]
        normed[:, cols(h)] = (m * inverse * scale).astype(BF16)
        gm[h] = (scale * g[:, cols(h)].astype(F32) * inverse - m * pull).astype(BF16)

        @pl.when(upper[6])
        def _():
            o[6, h] = far_grad(6, h)
            down_copy(6, h).start()

    def top(h):
        @pl.when(lower[6])
        def _():
            down_copy(6, h).wait_recv()
            cur[h] = got[6, h]

        @pl.when(upper[6])
        def _():
            cur[h] = jnp.zeros((WIDTH, WIDTH), F32)

        split(5, h)
        down_copy(5, h).start()

    def middle(b, h):
        down_copy(b, h).wait_recv()
        cur[h] = cur[h] + got[b, h]
        split(b - 1, h)
        down_copy(b - 1, h).start()

    def three(h):
        down_copy(3, h).wait_recv()
        cur[h] = cur[h] + got[3, h]
        split(2, h)

        @pl.when(is_inner)
        def _():
            join(2, h).start()
            split(1, h)

    def two_join(h):
        @pl.when(is_outer)
        def _():
            join(2, h).wait_recv()
            o[2, h] = o[2, h] + got_join[h]
            down_copy(2, h).start()

    def two(h):
        @pl.when(is_outer)
        def _():
            down_copy(2, h).wait_recv()
            cur[h] = cur[h] + got[2, h]
            split(1, h)
            join(1, h).start()
            split(0, h)
            down_copy(0, h).start()

    def one_join(h):
        @pl.when(is_inner)
        def _():
            join(1, h).wait_recv()
            o[1, h] = o[1, h] + got_join[h]
            down_copy(1, h).start()

    def one(h):
        @pl.when(is_inner)
        def _():
            down_copy(1, h).wait_recv()
            cur[h] = cur[h] + got[1, h]
            split(0, h)
            down_copy(0, h).start()

    def near_backward(h):
        grad = gm[h]
        query = q[:, cols(h)]
        gn = dot(v[:, cols(h)], grad, 1, 1)
        gs = (gn * weight[h]).astype(BF16)
        gkp[h] = dot(gs, query, 1, 0)
        gvp[h] = dot(near[h], grad, 1, 0)
        both = gn * score[h]
        level = table[...]
        for l in range(NEAR_LEVELS):
            part = jnp.sum(jnp.where(level == float(l), both, 0.0), axis=0, keepdims=True)
            gl[l, pl.ds(h, 1), :] = part * (2.0 ** (-max(l - 1, 0) / 2))
        mixed[h] = jnp.zeros((WIDTH, TOK), F32)
        query_t = q_t[h].astype(F32)
        for b in range(BITS):
            gl[NEAR_LEVELS + b, pl.ds(h, 1), :] = jnp.zeros((1, TOK), F32)

            @pl.when(upper[b])
            def _(b=b):
                read = dot(recv[b, h].astype(BF16), grad, 1, 1)
                mixed[h] = mixed[h] + read * far_row(b, h)
                part = jnp.sum(query_t * read, axis=0, keepdims=True) * reach[b:b + 1, :]
                gl[NEAR_LEVELS + b, pl.ds(h, 1), :] = part * (2.0 ** (-(7 + b) / 2))
        gq[:, cols(h)] = (dot(gs, k[:, cols(h)], 0, 0) + mixed[h].T).astype(BF16)

    def zero(h):
        down_copy(0, h).wait_recv()
        carried = (cur[h] + got[0, h]).astype(BF16)
        held = keep[...]
        kept_v = (v[:, cols(h)].astype(F32) * held).astype(BF16)
        kept_k = (k[:, cols(h)].astype(F32) * held).astype(BF16)
        gk[:, cols(h)] = (gkp[h] + dot(kept_v, carried, 1, 1)).astype(BF16)
        gv[:, cols(h)] = (gvp[h] + dot(kept_k, carried, 1, 0)).astype(BF16)

    events = (
        emit, top, functools.partial(middle, 5), functools.partial(middle, 4), three,
        two_join, two, one_join, one, zero,
    )

    @pl.loop(0, NH + DOWN_LAG[-1])
    def _(step):
        for lag, event in zip(DOWN_LAG, events):
            h = step - lag

            @pl.when((h >= 0) & (h < NH))
            def _(h=h, event=event):
                event(h)

        h = step - 1

        @pl.when((h >= 0) & (h < NH))
        def _():
            near_backward(h)

    swap.wait_send()
    for b in range(BITS):
        only(b, lambda b=b: gate_copy(b).wait_send())
    gate_relay(1).wait_send()

    @pl.loop(0, NH)
    def _(h):
        for b in range(BITS):
            only(b, lambda b=b: up_copy(b, h).wait_send())
        up_relay(1, h).wait_send()
        for b in (0, 3, 4, 5):
            down_copy(b, h).wait_send()
        pl.when(upper[6])(lambda: down_copy(6, h).wait_send())
        pl.when(is_outer)(lambda: down_copy(2, h).wait_send())
        pl.when(is_inner)(lambda: down_copy(1, h).wait_send())
        join(1, h).wait_send()


def per_device(queries, keys, values, segment, level_weight, gain, grad_out):
    segment = segment.astype(F32)
    places = jnp.arange(TOK, dtype=jnp.int32)
    crossed = jnp.bitwise_xor(places[:, None], places[None, :])
    levels = jnp.zeros((TOK, TOK), F32)
    for offset in range(NEAR_LEVELS - 1):
        levels = levels + (jnp.right_shift(crossed, offset) > 0).astype(F32)
    seen = (segment[:, None] == segment[None, :]) & (places[:, None] <= places[None, :])
    table = jnp.where(seen, levels, -1.0)
    keep = jnp.broadcast_to(jnp.where(segment == segment[-1], 1.0, 0.0)[:, None], (TOK, WIDTH))
    rows = jnp.stack([
        jnp.broadcast_to(segment[-1:], (8, TOK)), jnp.broadcast_to(segment[None, :], (8, TOK)),
    ])
    level_scale = jnp.exp2(-jnp.maximum(jnp.arange(LEVELS) - 1, 0).astype(F32) / 2.0)
    scaled = level_weight * level_scale[:, None, None]
    by_head = jnp.pad(scaled, ((0, 1), (0, 0), (0, 0))).transpose(1, 0, 2)

    vmem = pl.BlockSpec(memory_space=pltpu.VMEM)
    dma = pltpu.SemaphoreType.DMA
    square = (WIDTH, WIDTH)
    wide = jax.ShapeDtypeStruct((TOK, NH * WIDTH), BF16)
    return pl.pallas_call(
        body,
        name="levels",
        out_shape=(wide, wide, wide, wide, jax.ShapeDtypeStruct((LEVELS, NH, TOK), F32)),
        in_specs=[vmem] * 9,
        out_specs=(vmem,) * 5,
        scratch_shapes=[
            pltpu.VMEM((NH,) + square, F32),
            pltpu.VMEM((BITS, NH) + square, F32),
            pltpu.VMEM((BITS - 1, NH) + square, F32),
            pltpu.VMEM((BITS, 8, 128), F32),
            pltpu.VMEM((BITS, 8, 128), F32),
            pltpu.VMEM((8, 128), F32),
            pltpu.VMEM((NH,) + square, BF16),
            pltpu.VMEM((NH,) + square, BF16),
            pltpu.VMEM((NH,) + square, F32),
            pltpu.VMEM((NH,) + square, F32),
            pltpu.VMEM((NH,) + square, F32),
            pltpu.VMEM((2,) + square, F32),
            pltpu.VMEM((2,) + square, F32),
            pltpu.VMEM((NH,) + square, BF16),
            pltpu.VMEM((BITS, NH) + square, F32),
            pltpu.VMEM((BITS, NH) + square, F32),
            pltpu.VMEM((NH,) + square, F32),
            pltpu.VMEM((NH,) + square, F32),
            pltpu.VMEM((NH,) + square, F32),
            pltpu.VMEM((NH,) + square, F32),
            dma((BITS, NH)), dma((BITS, NH)), dma((NH,)), dma((BITS,)), dma((BITS,)), dma,
            dma((BITS, NH)), dma((BITS, NH)), dma((NH,)), dma((NH,)), dma, dma,
        ],
        compiler_params=pltpu.CompilerParams(
            collective_id=1, has_side_effects=True, vmem_limit_bytes=56 << 20),
    )(queries, keys, values, grad_out, by_head, rows, table, keep, gain[None, :])


def solution(mesh):
    placed = (
        P("tm", "head"), P("tm", "head"), P("tm", "head"), P("tm"),
        P(None, "head", "tm"), P("head"), P("tm", "head"),
    )
    return jax.shard_map(
        per_device,
        mesh=mesh,
        in_specs=placed,
        out_specs=(P("tm", "head"),) * 4 + (P(None, "head", "tm"),),
        check_vma=False,
    )
```

time: 515 us -> 241 us (0.47)
  the two profiles are of different devices: /device:TPU:1 before, /device:TPU:8 now
where the time goes in v1:
time: 241 us
  Pallas kernels  229 us (95%)
  local copies, waits for them, and re-layouts  9.9 us (4%)
    pallas_call x1, Pallas kernels, per_device(): pl.pallas_call(body, name='levels', out_shape=(wide, wide, wide, wide, ja...  229 us
    unnamed x17, local copies, waits for them, and re-layouts  6.69 us

profile of v1, /device:TPU:8, one launch (start us, length us, event | category | flops | bytes accessed | tf_op | source)
XLA Modules:
  0.0 240.9 jit_solution(10400779169235918676)
XLA Ops:
  0.6 0.0 copy-start.5
  0.6 0.0 copy-start.3
  0.7 0.6 copy-done.5
  1.3 0.6 slice.6
  1.9 0.6 compare_select_fusion
  2.6 1.2 stack.3.rows
  3.8 0.7 add_select_fusion.table
  4.5 0.7 broadcast_in_dim.32.keep
  5.2 0.0 copy-done.3
  5.2 0.1 copy_multiply_fusion
  5.3 0.7 pad_bitcast_fusion.lw
  6.0 228.8 %levels.1 = (bf16[128,2048]{1,0:T(8,128)(2,1)}, bf16[128,2048]{1,0:T(8,128)(2,1)}, bf16[128,2048]{1,0:T(8,128)(2,1)}, bf16[128,2048]{1,0:T(8,128)(2,1)}, f32[15,16,128]{2,1,0:T(8,128)}) custom-call(bf16[128,2048]{1,0:T(8,128)(2,1)} %q.1, bf16[128,2048]{1,0:T(8,128)(2,1)} %k.1, bf16[128,2048]{1,0:T(8,128)(2,1)} %v.1, bf16[128,2048]{1,0:T(8,128)(2,1)} %g.1, ...), custom_call_target="tpu_custom_call" | custom-call | tf_op jit(solution)/shard_map/levels/pallas_call | solution.py:383
  234.8 0.0 copy-start.2
  234.8 1.9 copy.21
  236.8 0.0 copy-done.2
  236.8 0.0 copy-start.1
  236.8 0.8 copy.22
  237.5 0.4 copy-done.1
  238.0 0.0 copy-start
  238.0 0.8 copy.23
  238.8 0.4 copy-done
  239.2 0.8 copy.24
  240.0 0.2 copy-done.4
  240.2 0.6 copy.25
  (4 shorter events, 0.0 us)
Async XLA Ops:
  0.6 0.7 copy-start.5
  0.6 4.6 %copy-start.3 = (f32[15,16,128]{2,1,0:T(8,128)S(1)}, f32[15,16,128]{2,1,0:T(8,128)}, u32[]{:S(2)}) copy-start(f32[15,16,128]{2,1,0:T(8,128)} %param.11) | copy-start | bytes 368644
  234.8 2.0 copy-start.2
  236.8 1.2 copy-start.1
  238.0 1.2 copy-start
  239.2 1.0 copy-start.4

commit v2 on v1

--- a/solution.py
+++ b/solution.py
@@ -17,8 +17,13 @@
 NEAR_LEVELS = 8
 LEVELS = NEAR_LEVELS + BITS
 FEATURES = 4096
-UP_LAG = (0, 3, 7, 10, 12, 14, 16)
-DOWN_LAG = (0, 1, 3, 5, 7, 9, 11, 13, 15, 17)
+UP_LAG = (0, (2, 4), (8, 6), 10, 12, 14, 16)
+AHEAD = 3
+DOWN_LAG = (0, 2, 4, 6, 8, 10, 12, 14, 16, 18)
+
+
+def level_scale(l):
+    return 2.0 ** (-max(l - 1, 0) / 2)
 
 
 def dot(a, b, left, right):
@@ -52,9 +57,9 @@
 
 
 def body(
-    q, k, v, g, lw, rows, table, keep, gain,
+    q, k, v, g, lw, segment, gain,
     normed, gq, gk, gv, gl,
-    tails, recv, agg, grecv, gagg, reach, q_t, near, score, weight, mixed, sums, sums_got,
+    table, keep, far, tails, recv, agg, grecv, gagg, reach, q_t, near, score, weight, mixed, sums, sums_got,
     gm, o, got, got_join, cur, gkp, gvp,
     ssem, rsem, lsem, gss, grs, gls, dssem, drsem, jss, jrs, xss, xrs,
 ):
@@ -100,14 +105,33 @@
     def gate_relay(b):
         return remote(grecv.at[b], grecv.at[b], gls, grs.at[b], target[0])
 
-    gagg[0] = rows[0]
-    gate_copy(0).start()
-
-    @pl.loop(0, NH)
-    def _(h):
+    def level_row(l, h):
+        return lw[l, pl.ds(h, 1), :] * level_scale(l)
+
+    def send_tail(h):
         kept = k[:, cols(h)].astype(F32) * keep[...]
         tails[h] = dot(kept.astype(BF16), v[:, cols(h)], 0, 0)
         up_copy(0, h).start()
+
+    row = segment[...].astype(F32)
+    last = row[:, TOK - 1:TOK]
+    gagg[0] = jnp.broadcast_to(last, (8, TOK))
+    gate_copy(0).start()
+    across_t = jnp.broadcast_to(row, (TOK, TOK))
+    down_s = across_t.T
+    keep[...] = jnp.where(down_s == last, 1.0, 0.0)
+
+    @pl.loop(0, AHEAD)
+    def _(h):
+        send_tail(h)
+
+    at_s = lax.broadcasted_iota(jnp.int32, (TOK, TOK), 0)
+    at_t = lax.broadcasted_iota(jnp.int32, (TOK, TOK), 1)
+    crossed = jnp.bitwise_xor(at_s, at_t)
+    levels = jnp.zeros((TOK, TOK), F32)
+    for offset in range(NEAR_LEVELS - 1):
+        levels = levels + jnp.where(crossed >= (1 << offset), 1.0, 0.0)
+    table[...] = jnp.where((down_s == across_t) & (at_s <= at_t), levels, -1.0)
 
     def near_forward(h):
         query = q[:, cols(h)]
@@ -115,7 +139,7 @@
         level = table[...]
         w = jnp.zeros((TOK, TOK), F32)
         for l in range(NEAR_LEVELS):
-            w = jnp.where(level == float(l), lw[h, l:l + 1, :], w)
+            w = jnp.where(level == float(l), level_row(l, h), w)
         terms = (s * w).astype(BF16)
         score[h] = s
         weight[h] = w
@@ -132,7 +156,7 @@
             if b < BITS - 1:
                 gagg[b + 1] = gagg[b] * upper_f[b] + grecv[b] * (1.0 - upper_f[b])
                 only(b + 1, lambda: gate_copy(b + 1).start())
-            hit = jnp.where(rows[1, 0:1, :] == grecv[b, 0:1, :], 1.0, 0.0)
+            hit = jnp.where(segment[...].astype(F32) == grecv[b, 0:1, :], 1.0, 0.0)
             reach[b:b + 1, :] = hit * upper_f[b]
 
         up_copy(b, h).wait_recv()
@@ -147,8 +171,9 @@
             only(b + 1, lambda: up_copy(b + 1, h).start())
 
     def far_read(h):
-        by = lw[h, 8:16, :] * reach[...]
-        by_t = by.T
+        for b in range(BITS):
+            far[b:b + 1, :] = level_row(NEAR_LEVELS + b, h)
+        by_t = (far[...] * reach[...]).T
         query = q[:, cols(h)].astype(F32)
         for b in range(BITS):
             @pl.when(upper[b])
@@ -161,11 +186,19 @@
 
     sums[...] = jnp.zeros_like(sums)
     reach[...] = jnp.zeros_like(reach)
+    far[...] = jnp.zeros_like(far)
 
     @pl.loop(0, NH + UP_LAG[-1])
     def _(step):
+        @pl.when(step + AHEAD < NH)
+        def _():
+            send_tail(step + AHEAD)
+
         for b in range(BITS):
-            h = step - UP_LAG[b]
+            lag = UP_LAG[b]
+            if isinstance(lag, tuple):
+                lag = lag[0] * inner + lag[1] * (1 - inner)
+            h = step - lag
 
             @pl.when((h >= 0) & (h < NH))
             def _(b=b, h=h):
@@ -197,7 +230,7 @@
         return remote(o.at[b, h], got_join.at[h], jss.at[h], jrs.at[h], target[0])
 
     def far_row(b, h):
-        return lw[h, 8 + b:9 + b, :] * reach[b:b + 1, :]
+        return level_row(NEAR_LEVELS + b, h) * reach[b:b + 1, :]
 
     def far_grad(b, h):
         scaled_q = (q_t[h].astype(F32) * far_row(b, h)).astype(BF16)
@@ -298,7 +331,7 @@
         level = table[...]
         for l in range(NEAR_LEVELS):
             part = jnp.sum(jnp.where(level == float(l), both, 0.0), axis=0, keepdims=True)
-            gl[l, pl.ds(h, 1), :] = part * (2.0 ** (-max(l - 1, 0) / 2))
+            gl[l, pl.ds(h, 1), :] = part * level_scale(l)
         mixed[h] = jnp.zeros((WIDTH, TOK), F32)
         query_t = q_t[h].astype(F32)
         for b in range(BITS):
@@ -309,7 +342,7 @@
                 read = dot(recv[b, h].astype(BF16), grad, 1, 1)
                 mixed[h] = mixed[h] + read * far_row(b, h)
                 part = jnp.sum(query_t * read, axis=0, keepdims=True) * reach[b:b + 1, :]
-                gl[NEAR_LEVELS + b, pl.ds(h, 1), :] = part * (2.0 ** (-(7 + b) / 2))
+                gl[NEAR_LEVELS + b, pl.ds(h, 1), :] = part * level_scale(NEAR_LEVELS + b)
         gq[:, cols(h)] = (dot(gs, k[:, cols(h)], 0, 0) + mixed[h].T).astype(BF16)
 
     def zero(h):
@@ -360,22 +393,6 @@
 
 
 def per_device(queries, keys, values, segment, level_weight, gain, grad_out):
-    segment = segment.astype(F32)
-    places = jnp.arange(TOK, dtype=jnp.int32)
-    crossed = jnp.bitwise_xor(places[:, None], places[None, :])
-    levels = jnp.zeros((TOK, TOK), F32)
-    for offset in range(NEAR_LEVELS - 1):
-        levels = levels + (jnp.right_shift(crossed, offset) > 0).astype(F32)
-    seen = (segment[:, None] == segment[None, :]) & (places[:, None] <= places[None, :])
-    table = jnp.where(seen, levels, -1.0)
-    keep = jnp.broadcast_to(jnp.where(segment == segment[-1], 1.0, 0.0)[:, None], (TOK, WIDTH))
-    rows = jnp.stack([
-        jnp.broadcast_to(segment[-1:], (8, TOK)), jnp.broadcast_to(segment[None, :], (8, TOK)),
-    ])
-    level_scale = jnp.exp2(-jnp.maximum(jnp.arange(LEVELS) - 1, 0).astype(F32) / 2.0)
-    scaled = level_weight * level_scale[:, None, None]
-    by_head = jnp.pad(scaled, ((0, 1), (0, 0), (0, 0))).transpose(1, 0, 2)
-
     vmem = pl.BlockSpec(memory_space=pltpu.VMEM)
     dma = pltpu.SemaphoreType.DMA
     square = (WIDTH, WIDTH)
@@ -384,9 +401,12 @@
         body,
         name="levels",
         out_shape=(wide, wide, wide, wide, jax.ShapeDtypeStruct((LEVELS, NH, TOK), F32)),
-        in_specs=[vmem] * 9,
+        in_specs=[vmem] * 7,
         out_specs=(vmem,) * 5,
         scratch_shapes=[
+            pltpu.VMEM(square, F32),
+            pltpu.VMEM(square, F32),
+            pltpu.VMEM((8, TOK), F32),
             pltpu.VMEM((NH,) + square, F32),
             pltpu.VMEM((BITS, NH) + square, F32),
             pltpu.VMEM((BITS - 1, NH) + square, F32),
@@ -412,7 +432,7 @@
         ],
         compiler_params=pltpu.CompilerParams(
             collective_id=1, has_side_effects=True, vmem_limit_bytes=56 << 20),
-    )(queries, keys, values, grad_out, by_head, rows, table, keep, gain[None, :])
+    )(queries, keys, values, grad_out, level_weight, segment[None, :], gain[None, :])
 
 
 def solution(mesh):

time: 241 us -> 173 us (0.72)
  Pallas kernels: 229 us -> 166 us
  local copies, waits for them, and re-layouts: 9.9 us -> 6.05 us
    pallas_call x1, Pallas kernels: 229 us -> 166 us  [per_device(): pl.pallas_call(body, name='levels', out_shape=(wide, wide, wide, wide, ja...]
    unnamed x17 -> x13, local copies, waits for them, and re-layouts: 6.69 us -> 6.05 us
where the time goes in v2:
time: 173 us; the launch traced here: 172 us
  Pallas kernels  166 us (96%)
  local copies, waits for them, and re-layouts  6.05 us (3%)
    pallas_call x1, Pallas kernels, per_device(): pl.pallas_call(body, name='levels', out_shape=(wide, wide, wide, wide, ja...  166 us
    unnamed x13, local copies, waits for them, and re-layouts  6.05 us

profile of v2, /device:TPU:8, one launch (start us, length us, event | category | flops | bytes accessed | tf_op | source)
XLA Modules:
  0.0 172.4 jit_solution(8990895642704271733)
XLA Ops:
  0.6 165.7 %levels.1 = (bf16[128,2048]{1,0:T(8,128)(2,1)}, bf16[128,2048]{1,0:T(8,128)(2,1)}, bf16[128,2048]{1,0:T(8,128)(2,1)}, bf16[128,2048]{1,0:T(8,128)(2,1)}, f32[15,16,128]{2,1,0:T(8,128)}) custom-call(bf16[128,2048]{1,0:T(8,128)(2,1)} %q.1, bf16[128,2048]{1,0:T(8,128)(2,1)} %k.1, bf16[128,2048]{1,0:T(8,128)(2,1)} %v.1, bf16[128,2048]{1,0:T(8,128)(2,1)} %g.1, ...), custom_call_target="tpu_custom_call" | custom-call | tf_op jit(solution)/shard_map/levels/pallas_call | solution.py:400
  166.3 0.0 copy-start.2
  166.3 1.9 %copy.17 = bf16[128,2048]{1,0:T(8,128)(2,1)} copy(bf16[128,2048]{1,0:T(8,128)(2,1)} %get-tuple-element.10) | data formatting | bytes 1048576
  168.2 0.0 copy-done.2
  168.2 0.0 copy-start.1
  168.3 0.8 copy.18
  169.0 0.4 copy-done.1
  169.5 0.0 copy-start
  169.5 0.8 copy.19
  170.3 0.4 copy-done
  170.7 0.0 copy-start.3
  170.7 0.8 copy.20
  171.5 0.2 copy-done.3
  171.7 0.6 copy.21
Async XLA Ops:
  166.3 2.0 %copy-start.2 = (bf16[128,2048]{1,0:T(8,128)(2,1)S(1)}, bf16[128,2048]{1,0:T(8,128)(2,1)}, u32[]{:S(2)}) copy-start(bf16[128,2048]{1,0:T(8,128)(2,1)} %get-tuple-element.11) | copy-start | bytes 1572868
  168.2 1.2 copy-start.1
  169.5 1.2 copy-start
  170.7 1.0 copy-start.3

commit v3 on v2

--- a/solution.py
+++ b/solution.py
@@ -19,7 +19,7 @@
 FEATURES = 4096
 UP_LAG = (0, (2, 4), (8, 6), 10, 12, 14, 16)
 AHEAD = 3
-DOWN_LAG = (0, 2, 4, 6, 8, 10, 12, 14, 16, 18)
+DOWN_LAG = (0, 2, 4, 6, 8, 10, 12, 14, 16, 16, (19, 18))
 
 
 def level_scale(l):
@@ -57,12 +57,21 @@
 
 
 def body(
-    q, k, v, g, lw, segment, gain,
-    normed, gq, gk, gv, gl,
+    q_in, k_in, v_in, g_in, lw_in, segment, gain,
+    normed_out, gq_out, gk_out, gv_out, gl_out,
+    q, k, v, g, lw, normed, gq, gk, gv, gl,
     table, keep, far, tails, recv, agg, grecv, gagg, reach, q_t, near, score, weight, mixed, sums, sums_got,
     gm, o, got, got_join, cur, gkp, gvp,
-    ssem, rsem, lsem, gss, grs, gls, dssem, drsem, jss, jrs, xss, xrs,
+    ssem, rsem, lsem, gss, grs, gls, dssem, drsem, jss, jrs, xss, xrs, in_sem, out_sem, gl_sem,
 ):
+    loads = [
+        pltpu.make_async_copy(source, held, in_sem.at[i])
+        for i, (source, held) in enumerate(
+            ((k_in, k), (v_in, v), (q_in, q), (lw_in, lw), (g_in, g))
+        )
+    ]
+    for load in loads:
+        load.start()
     inner, partners, bits = place()
     near_by, across, x_one, x_three, y_one, y_three = partners
     other_core = {"head": 1 - lax.axis_index("head")}
@@ -84,6 +93,12 @@
     def cols(h):
         return pl.ds(pl.multiple_of(h * WIDTH, WIDTH), WIDTH)
 
+    def place_out(n, h):
+        held, out = ((normed, normed_out), (gq, gq_out), (gk, gk_out), (gv, gv_out))[n]
+        return pltpu.make_async_copy(held.at[:, cols(h)], out.at[:, cols(h)], out_sem.at[n, h])
+
+    place_levels = pltpu.make_async_copy(gl, gl_out, gl_sem)
+
     def only(b, fn):
         if b == 1:
             pl.when(is_inner)(fn)
@@ -120,6 +135,9 @@
     across_t = jnp.broadcast_to(row, (TOK, TOK))
     down_s = across_t.T
     keep[...] = jnp.where(down_s == last, 1.0, 0.0)
+
+    loads[0].wait()
+    loads[1].wait()
 
     @pl.loop(0, AHEAD)
     def _(h):
@@ -184,6 +202,8 @@
         sums[0] = sums[0] + m * m
         sums[1] = sums[1] + m * g[:, cols(h)].astype(F32) * gain[:, cols(h)]
 
+    for load in loads[2:]:
+        load.wait()
     sums[...] = jnp.zeros_like(sums)
     reach[...] = jnp.zeros_like(reach)
     far[...] = jnp.zeros_like(far)
@@ -252,6 +272,7 @@
         m = mixed[h]
         scale = gain[:, cols(h)]
         normed[:, cols(h)] = (m * inverse * scale).astype(BF16)
+        place_out(0, h).start()
         gm[h] = (scale * g[:, cols(h)].astype(F32) * inverse - m * pull).astype(BF16)
 
         @pl.when(upper[6])
@@ -303,6 +324,10 @@
             split(1, h)
             join(1, h).start()
             split(0, h)
+
+    def late(h):
+        @pl.when(is_outer)
+        def _():
             down_copy(0, h).start()
 
     def one_join(h):
@@ -344,6 +369,11 @@
                 part = jnp.sum(query_t * read, axis=0, keepdims=True) * reach[b:b + 1, :]
                 gl[NEAR_LEVELS + b, pl.ds(h, 1), :] = part * level_scale(NEAR_LEVELS + b)
         gq[:, cols(h)] = (dot(gs, k[:, cols(h)], 0, 0) + mixed[h].T).astype(BF16)
+        place_out(1, h).start()
+
+        @pl.when(h == NH - 1)
+        def _():
+            place_levels.start()
 
     def zero(h):
         down_copy(0, h).wait_recv()
@@ -353,15 +383,19 @@
         kept_k = (k[:, cols(h)].astype(F32) * held).astype(BF16)
         gk[:, cols(h)] = (gkp[h] + dot(kept_v, carried, 1, 1)).astype(BF16)
         gv[:, cols(h)] = (gvp[h] + dot(kept_k, carried, 1, 0)).astype(BF16)
+        place_out(2, h).start()
+        place_out(3, h).start()
 
     events = (
         emit, top, functools.partial(middle, 5), functools.partial(middle, 4), three,
-        two_join, two, one_join, one, zero,
+        two_join, two, one_join, one, late, zero,
     )
 
-    @pl.loop(0, NH + DOWN_LAG[-1])
+    @pl.loop(0, NH + max(DOWN_LAG[-1]))
     def _(step):
         for lag, event in zip(DOWN_LAG, events):
+            if isinstance(lag, tuple):
+                lag = lag[0] * inner + lag[1] * (1 - inner)
             h = step - lag
 
             @pl.when((h >= 0) & (h < NH))
@@ -374,6 +408,7 @@
         def _():
             near_backward(h)
 
+    place_levels.wait()
     swap.wait_send()
     for b in range(BITS):
         only(b, lambda b=b: gate_copy(b).wait_send())
@@ -390,6 +425,13 @@
         pl.when(is_outer)(lambda: down_copy(2, h).wait_send())
         pl.when(is_inner)(lambda: down_copy(1, h).wait_send())
         join(1, h).wait_send()
+        for n in range(4):
+            place_out(n, h).wait()
+
+
+def hand_over(*refs):
+    for source, out in zip(refs[:5], refs[5:]):
+        out[...] = source[...]
 
 
 def per_device(queries, keys, values, segment, level_weight, gain, grad_out):
@@ -397,13 +439,25 @@
     dma = pltpu.SemaphoreType.DMA
     square = (WIDTH, WIDTH)
     wide = jax.ShapeDtypeStruct((TOK, NH * WIDTH), BF16)
-    return pl.pallas_call(
+    away = pl.BlockSpec(memory_space=pl.ANY)
+    shapes = (wide, wide, wide, wide, jax.ShapeDtypeStruct((LEVELS, NH, TOK), F32))
+    made = pl.pallas_call(
         body,
         name="levels",
-        out_shape=(wide, wide, wide, wide, jax.ShapeDtypeStruct((LEVELS, NH, TOK), F32)),
-        in_specs=[vmem] * 7,
-        out_specs=(vmem,) * 5,
+        out_shape=shapes,
+        in_specs=[away] * 5 + [vmem] * 2,
+        out_specs=(away,) * 5,
         scratch_shapes=[
+            pltpu.VMEM((TOK, NH * WIDTH), BF16),
+            pltpu.VMEM((TOK, NH * WIDTH), BF16),
+            pltpu.VMEM((TOK, NH * WIDTH), BF16),
+            pltpu.VMEM((TOK, NH * WIDTH), BF16),
+            pltpu.VMEM((LEVELS, NH, TOK), F32),
+            pltpu.VMEM((TOK, NH * WIDTH), BF16),
+            pltpu.VMEM((TOK, NH * WIDTH), BF16),
+            pltpu.VMEM((TOK, NH * WIDTH), BF16),
+            pltpu.VMEM((TOK, NH * WIDTH), BF16),
+            pltpu.VMEM((LEVELS, NH, TOK), F32),
             pltpu.VMEM(square, F32),
             pltpu.VMEM(square, F32),
             pltpu.VMEM((8, TOK), F32),
@@ -429,10 +483,21 @@
             pltpu.VMEM((NH,) + square, F32),
             dma((BITS, NH)), dma((BITS, NH)), dma((NH,)), dma((BITS,)), dma((BITS,)), dma,
             dma((BITS, NH)), dma((BITS, NH)), dma((NH,)), dma((NH,)), dma, dma,
+            dma((5,)), dma((4, NH)), dma,
         ],
         compiler_params=pltpu.CompilerParams(
             collective_id=1, has_side_effects=True, vmem_limit_bytes=56 << 20),
     )(queries, keys, values, grad_out, level_weight, segment[None, :], gain[None, :])
+    strip = pl.BlockSpec((TOK // 4, NH * WIDTH), lambda i: (i, 0))
+    whole = pl.BlockSpec((LEVELS, NH, TOK), lambda i: (0, 0, 0))
+    return pl.pallas_call(
+        hand_over,
+        name="hand_over",
+        grid=(4,),
+        out_shape=shapes,
+        in_specs=[strip] * 4 + [whole],
+        out_specs=[strip] * 4 + [whole],
+    )(*made)
 
 
 def solution(mesh):

time: 173 us -> 169 us (0.977)
  local copies, waits for them, and re-layouts: 6.05 us -> 0 us
    unnamed x13 -> x0, local copies, waits for them, and re-layouts: 6.05 us -> none
    pallas_call x1 -> x2, Pallas kernels: 166 us -> 166 us  [the longest x1 162 us: per_device(): pl.pallas_call(body, name='levels', out_shape=shapes, in_specs=[away] * 5...]
where the time goes in v3:
time: 169 us; the launch traced here: 167 us
  Pallas kernels  166 us (98%)
    pallas_call x1, Pallas kernels, per_device(): pl.pallas_call(body, name='levels', out_shape=shapes, in_specs=[away] * 5...  162 us
    pallas_call x1, Pallas kernels, per_device(): pl.pallas_call(hand_over, name='hand_over', grid=(4,), out_shape=shapes,...  4.03 us

profile of v3, /device:TPU:8, one launch (start us, length us, event | category | flops | bytes accessed | tf_op | source)
XLA Modules:
  0.0 167.0 jit_solution(600632659712623798)
XLA Ops:
  0.6 162.3 %levels.1 = (bf16[128,2048]{1,0:T(8,128)(2,1)}, bf16[128,2048]{1,0:T(8,128)(2,1)}, bf16[128,2048]{1,0:T(8,128)(2,1)}, bf16[128,2048]{1,0:T(8,128)(2,1)}, f32[15,16,128]{2,1,0:T(8,128)}) custom-call(bf16[128,2048]{1,0:T(8,128)(2,1)} %q_in.1, bf16[128,2048]{1,0:T(8,128)(2,1)} %k_in.1, bf16[128,2048]{1,0:T(8,128)(2,1)} %v_in.1, bf16[128,2048]{1,0:T(8,128)(2,1)} %g_in.1, ...), custom_call_target="tpu_custom_call" | custom-call | tf_op jit(solution)/shard_map/levels/pallas_call | solution.py:444
  162.9 4.0 %hand_over.1 = (bf16[128,2048]{1,0:T(8,128)(2,1)}, bf16[128,2048]{1,0:T(8,128)(2,1)}, bf16[128,2048]{1,0:T(8,128)(2,1)}, bf16[128,2048]{1,0:T(8,128)(2,1)}, f32[15,16,128]{2,1,0:T(8,128)}) custom-call(bf16[128,2048]{1,0:T(8,128)(2,1)} %get-tuple-element.10.refs_0_, bf16[128,2048]{1,0:T(8,128)(2,1)} %get-tuple-element.11.refs_1_, ...), custom_call_target="tpu_custom_call" | custom-call | tf_op jit(solution)/shard_map/hand_over/pallas_call | solution.py:493

commit v4 on v3

--- a/solution.py
+++ b/solution.py
@@ -193,12 +193,11 @@
             far[b:b + 1, :] = level_row(NEAR_LEVELS + b, h)
         by_t = (far[...] * reach[...]).T
         query = q[:, cols(h)].astype(F32)
+        m = mixed[h]
         for b in range(BITS):
-            @pl.when(upper[b])
-            def _(b=b):
-                scaled_q = (query * by_t[:, b:b + 1]).astype(BF16)
-                mixed[h] = mixed[h] + dot(scaled_q, recv[b, h].astype(BF16), 1, 0)
-        m = mixed[h]
+            scaled_q = (query * by_t[:, b:b + 1]).astype(BF16)
+            m = m + dot(scaled_q, recv[b, h].astype(BF16), 1, 0)
+        mixed[h] = m
         sums[0] = sums[0] + m * m
         sums[1] = sums[1] + m * g[:, cols(h)].astype(F32) * gain[:, cols(h)]
 
@@ -258,15 +257,11 @@
 
     def split(b, h):
         same = jnp.where(grecv[b, 0:1, :] == gagg[b, 0:1, :], 1.0, 0.0)
-
-        @pl.when(upper[b])
-        def _():
-            o[b, h] = cur[h] * same + far_grad(b, h)
-
-        @pl.when(lower[b])
-        def _():
-            o[b, h] = cur[h]
-            cur[h] = cur[h] * same
+        leave_by = upper_f[b] * same + (1.0 - upper_f[b])
+        stay_by = upper_f[b] + (1.0 - upper_f[b]) * same
+        carried = cur[h]
+        o[b, h] = o[b, h] + carried * leave_by
+        cur[h] = carried * stay_by
 
     def emit(h):
         m = mixed[h]
@@ -275,10 +270,10 @@
         place_out(0, h).start()
         gm[h] = (scale * g[:, cols(h)].astype(F32) * inverse - m * pull).astype(BF16)
 
-        @pl.when(upper[6])
-        def _():
-            o[6, h] = far_grad(6, h)
-            down_copy(6, h).start()
+        for b in reversed(range(BITS)):
+            o[b, h] = far_grad(b, h)
+            if b == BITS - 1:
+                pl.when(upper[6])(lambda: down_copy(6, h).start())
 
     def top(h):
         @pl.when(lower[6])
@@ -357,18 +352,14 @@
         for l in range(NEAR_LEVELS):
             part = jnp.sum(jnp.where(level == float(l), both, 0.0), axis=0, keepdims=True)
             gl[l, pl.ds(h, 1), :] = part * level_scale(l)
-        mixed[h] = jnp.zeros((WIDTH, TOK), F32)
+        far_t = jnp.zeros((WIDTH, TOK), F32)
         query_t = q_t[h].astype(F32)
         for b in range(BITS):
-            gl[NEAR_LEVELS + b, pl.ds(h, 1), :] = jnp.zeros((1, TOK), F32)
-
-            @pl.when(upper[b])
-            def _(b=b):
-                read = dot(recv[b, h].astype(BF16), grad, 1, 1)
-                mixed[h] = mixed[h] + read * far_row(b, h)
-                part = jnp.sum(query_t * read, axis=0, keepdims=True) * reach[b:b + 1, :]
-                gl[NEAR_LEVELS + b, pl.ds(h, 1), :] = part * level_scale(NEAR_LEVELS + b)
-        gq[:, cols(h)] = (dot(gs, k[:, cols(h)], 0, 0) + mixed[h].T).astype(BF16)
+            read = dot(recv[b, h].astype(BF16), grad, 1, 1)
+            far_t = far_t + read * far_row(b, h)
+            part = jnp.sum(query_t * read, axis=0, keepdims=True) * reach[b:b + 1, :]
+            gl[NEAR_LEVELS + b, pl.ds(h, 1), :] = part * level_scale(NEAR_LEVELS + b)
+        gq[:, cols(h)] = (dot(gs, k[:, cols(h)], 0, 0) + far_t.T).astype(BF16)
         place_out(1, h).start()
 
         @pl.when(h == NH - 1)
@@ -430,8 +421,16 @@
 
 
 def hand_over(*refs):
-    for source, out in zip(refs[:5], refs[5:]):
-        out[...] = source[...]
+    held, read_sem, write_sem = refs[10:15], refs[15], refs[16]
+    reads = [pltpu.make_async_copy(refs[i], held[i], read_sem.at[i]) for i in range(5)]
+    writes = [pltpu.make_async_copy(held[i], refs[5 + i], write_sem.at[i]) for i in range(5)]
+    for read in reads:
+        read.start()
+    for read, write in zip(reads, writes):
+        read.wait()
+        write.start()
+    for write in writes:
+        write.wait()
 
 
 def per_device(queries, keys, values, segment, level_weight, gain, grad_out):
@@ -488,15 +487,13 @@
         compiler_params=pltpu.CompilerParams(
             collective_id=1, has_side_effects=True, vmem_limit_bytes=56 << 20),
     )(queries, keys, values, grad_out, level_weight, segment[None, :], gain[None, :])
-    strip = pl.BlockSpec((TOK // 4, NH * WIDTH), lambda i: (i, 0))
-    whole = pl.BlockSpec((LEVELS, NH, TOK), lambda i: (0, 0, 0))
     return pl.pallas_call(
         hand_over,
         name="hand_over",
-        grid=(4,),
         out_shape=shapes,
-        in_specs=[strip] * 4 + [whole],
-        out_specs=[strip] * 4 + [whole],
+        in_specs=[away] * 5,
+        out_specs=(away,) * 5,
+        scratch_shapes=[pltpu.VMEM(shape.shape, shape.dtype) for shape in shapes] + [dma((5,)), dma((5,))],
     )(*made)
 
 

time: 169 us -> 162 us (0.959); the launches traced: 167 us -> 162 us
  Pallas kernels: 166 us -> 161 us
    pallas_call x1, Pallas kernels: 162 us -> 159 us  [per_device(): pl.pallas_call(body, name='levels', out_shape=shapes, in_specs=[away] * 5...]
where the time goes in v4:
time: 162 us
  Pallas kernels  161 us (99%)
    pallas_call x1, Pallas kernels, per_device(): pl.pallas_call(body, name='levels', out_shape=shapes, in_specs=[away] * 5...  159 us

profile of v4, /device:TPU:8, one launch (start us, length us, event | category | flops | bytes accessed | tf_op | source)
XLA Modules:
  0.0 161.9 jit_solution(13882828133269370620)
XLA Ops:
  0.6 158.8 %levels.1 = (bf16[128,2048]{1,0:T(8,128)(2,1)}, bf16[128,2048]{1,0:T(8,128)(2,1)}, bf16[128,2048]{1,0:T(8,128)(2,1)}, bf16[128,2048]{1,0:T(8,128)(2,1)}, f32[15,16,128]{2,1,0:T(8,128)}) custom-call(bf16[128,2048]{1,0:T(8,128)(2,1)} %q_in.1, bf16[128,2048]{1,0:T(8,128)(2,1)} %k_in.1, bf16[128,2048]{1,0:T(8,128)(2,1)} %v_in.1, bf16[128,2048]{1,0:T(8,128)(2,1)} %g_in.1, ...), custom_call_target="tpu_custom_call" | custom-call | tf_op jit(solution)/shard_map/levels/pallas_call | solution.py:443
  159.5 2.5 %hand_over.1 = (bf16[128,2048]{1,0:T(8,128)(2,1)}, bf16[128,2048]{1,0:T(8,128)(2,1)}, bf16[128,2048]{1,0:T(8,128)(2,1)}, bf16[128,2048]{1,0:T(8,128)(2,1)}, f32[15,16,128]{2,1,0:T(8,128)}) custom-call(bf16[128,2048]{1,0:T(8,128)(2,1)} %get-tuple-element.10.refs_0_, bf16[128,2048]{1,0:T(8,128)(2,1)} %get-tuple-element.11.refs_1_, ...), custom_call_target="tpu_custom_call" | custom-call | tf_op jit(solution)/shard_map/hand_over/pallas_call | solution.py:490
